TPU v7x, 32 devices: a whole 2x2x4 slice. The times are simulated.
32 devices in a mesh: row: 8 (over z, x), col: 4 (over y, core).
Axes of the slice: x: 2, y: 2, z: 4, core: 2. Of those that a mesh axis runs over, the one named last changes fastest.
Arguments:
- eigvecs: bfloat16 [49152, 4096], P('row', 'col'), may hold values from -41 to 41
- reflectors: bfloat16 [8, 49152, 128], P(None, 'row'), as said below
- factors: float32 [8, 128, 128], replicated, as said below
Outputs:
- vectors: bfloat16 [49152, 4096], P('row', 'col')
- deviation: float32 [4096], P('col')
Inputs may be any that keep to these rules, and one draw needn't show every extreme that they name: `reflectors`: each panel's vectors are dense and linearly independent. factors[k] is the upper triangular compact WY factor of reflectors[k]: its inverse plus its inverse's transpose equals reflectors[k]^T reflectors[k], so that I - reflectors[k] factors[k] reflectors[k]^T is orthogonal up to rounding.
All inputs are finite; a program needn't handle non-finite values.
Results may differ from a plain program's by a relative error of at most 0.014.
Values may be sent and summed in bfloat16 or wider, within the bound.
A program may use at most 128 MiB of HBM per device.

v0:
```python
import jax
import jax.numpy as jnp
from jax import lax
from jax.sharding import PartitionSpec as P

NORD = 49152


def body(eigvecs, reflectors, factors):
    vectors = eigvecs
    panels = reflectors.shape[0]
    width = reflectors.shape[2]
    local_rows = reflectors.shape[1]
    stacked = jnp.transpose(reflectors, (1, 0, 2)).reshape(local_rows, panels * width)
    local_proj = lax.dot_general(
        stacked, eigvecs, (((0,), (0,)), ((), ())), preferred_element_type=jnp.float32
    )
    local_gram = lax.dot_general(
        stacked, stacked, (((0,), (0,)), ((), ())), preferred_element_type=jnp.float32
    )
    total_proj, total_gram = (
        lax.psum(local_proj.astype(jnp.bfloat16), "row").astype(jnp.float32),
        lax.psum(local_gram.astype(jnp.bfloat16), "row").astype(jnp.float32),
    )
    earlier = []
    for panel in range(panels):
        proj = total_proj[panel * width : (panel + 1) * width]
        for prior in range(panel):
            cross = total_gram[
                panel * width : (panel + 1) * width, prior * width : (prior + 1) * width
            ]
            proj = proj - jnp.dot(
                cross, earlier[prior].astype(jnp.float32), precision=lax.Precision.HIGHEST
            )
        scaled = jnp.dot(factors[panel], proj, precision=lax.Precision.HIGHEST).astype(jnp.bfloat16)
        earlier.append(scaled)
        update = jnp.dot(reflectors[panel], scaled, preferred_element_type=jnp.float32)
        vectors = (vectors.astype(jnp.float32) - update).astype(jnp.bfloat16)
    wide = vectors.astype(jnp.float32)
    local_squares = jnp.sum(wide * wide, axis=0)
    squares = lax.psum(local_squares, "row")
    deviation = jnp.sqrt(squares / NORD) - 1.0
    return (vectors, deviation)


def solution(mesh):
    placed = (P("row", "col"), P(None, "row", None), P())
    return jax.shard_map(
        body, mesh=mesh, in_specs=placed, out_specs=(P("row", "col"), P("col")), check_vma=False
    )
```

profile of v0, /device:TPU:0, one launch (start us, length us, event | category | flops | bytes accessed | tf_op | source)
XLA Modules:
  0.0 387.1 jit_solution(8457546555832240318)
XLA Ops:
  7.2 16.6 %copy.8 = bf16[8,6144,128]{1,2,0:T(8,128)(2,1)} copy(bf16[8,6144,128]{2,1,0:T(8,128)(2,1)} %param.4) | data formatting | bytes 25165824 | tf_op args[1]
  23.8 19.0 %convolution_convert_fusion = bf16[1024,1024]{1,0:T(8,128)(2,1)} fusion(bf16[6144,1024]{0,1:T(8,128)(2,1)} %bitcast.132), kind=kOutput, calls=%fused_computation.17 | convolution fusion | flops 12885950464 | bytes 14680064 | tf_op jit(solution)/shard_map/dot_general | solution.py:18
  42.8 16.9 %convolution_convert_fusion.1 = bf16[1024,1024]{1,0:T(8,128)(2,1)} fusion(bf16[6144,1024]{0,1:T(8,128)(2,1)} %bitcast.133, bf16[6144,1024]{1,0:T(8,128)(2,1)S(1)} %copy-done), kind=kOutput, calls=%fused_computation.18 | convolution fusion | flops 12885950464 | bytes 27262976 | tf_op jit(solution)/shard_map/dot_general | solution.py:15
  59.7 16.2 %copy.7 = bf16[6144,1024]{0,1:T(8,128)(2,1)} copy(bf16[6144,1024]{1,0:T(8,128)(2,1)} %param.3) | data formatting | bytes 25165824 | tf_op args[0]
  75.9 143.1 %all-reduce.3.cloned.1.call-done = (bf16[1024,1024]{1,0:T(8,128)(2,1)}, bf16[1024,1024]{1,0:T(8,128)(2,1)}) async-done(((bf16[1024,1024]{1,0:T(8,128)(2,1)}, bf16[1024,1024]{1,0:T(8,128)(2,1)}), (bf16[1024,1024]{1,0:T(8,128)(2,1)}, bf16[1024,1024]{1,0:T(8,128)(2,1)})) %all-reduce.3.cloned.1.call-update) | async-done | bytes 4194320 | tf_op jit(solution)/shard_map/psum | solution.py:22
  219.0 2.0 convert_element_type.126
  223.5 1.8 convolution_subtract_fusion.26
  230.2 1.8 convolution_convert_fusion.8
  232.1 9.8 %fusion.7 = bf16[6144,1024]{0,1:T(8,128)(2,1)} fusion(bf16[6144,1024]{0,1:T(8,128)(2,1)} %copy.7, bf16[1024,128]{1,0:T(8,128)(2,1)S(1)} %convolution_convert_fusion.9, bf16[8,6144,128]{2,1,0:T(8,128)(2,1)} %param.4), kind=kOutput, calls=%fused_computation.15 | convolution fusion | flops 1629487104 | bytes 27000832 | tf_op jit(solution)/shard_map/dot_general | solution.py:37
  241.9 9.8 %fusion.6 = bf16[6144,1024]{0,1:T(8,128)(2,1)} fusion(bf16[6144,1024]{0,1:T(8,128)(2,1)} %fusion.7, bf16[1024,128]{1,0:T(8,128)(2,1)S(1)} %convolution_convert_fusion.8, bf16[8,6144,128]{2,1,0:T(8,128)(2,1)} %param.4), kind=kOutput, calls=%fused_computation.13 | convolution fusion | flops 1629487104 | bytes 27000832 | tf_op jit(solution)/shard_map/dot_general | solution.py:37
  253.0 1.8 convolution_convert_fusion.7
  256.6 9.9 %fusion.5 = bf16[6144,1024]{0,1:T(8,128)(2,1)} fusion(bf16[6144,1024]{0,1:T(8,128)(2,1)} %fusion.6, bf16[1024,128]{1,0:T(8,128)(2,1)S(1)} %convolution_convert_fusion.7, bf16[8,6144,128]{2,1,0:T(8,128)(2,1)} %param.4), kind=kOutput, calls=%fused_computation.11 | convolution fusion | flops 1629487104 | bytes 27000832 | tf_op jit(solution)/shard_map/dot_general | solution.py:37
  267.4 1.8 convolution_convert_fusion.6
  271.3 9.8 %fusion.4 = bf16[6144,1024]{0,1:T(8,128)(2,1)} fusion(bf16[6144,1024]{0,1:T(8,128)(2,1)} %fusion.5, bf16[1024,128]{1,0:T(8,128)(2,1)S(1)} %convolution_convert_fusion.6, bf16[8,6144,128]{2,1,0:T(8,128)(2,1)} %param.4), kind=kOutput, calls=%fused_computation.9 | convolution fusion | flops 1629487104 | bytes 27000832 | tf_op jit(solution)/shard_map/dot_general | solution.py:37
  282.1 1.8 convolution_convert_fusion.5
  286.9 9.8 %fusion.3 = bf16[6144,1024]{0,1:T(8,128)(2,1)} fusion(bf16[6144,1024]{0,1:T(8,128)(2,1)} %fusion.4, bf16[1024,128]{1,0:T(8,128)(2,1)S(1)} %convolution_convert_fusion.5, bf16[8,6144,128]{2,1,0:T(8,128)(2,1)} %param.4), kind=kOutput, calls=%fused_computation.7 | convolution fusion | flops 1629487104 | bytes 27000832 | tf_op jit(solution)/shard_map/dot_general | solution.py:37
  297.7 1.8 convolution_convert_fusion.4
  303.5 9.8 %fusion.2 = bf16[6144,1024]{0,1:T(8,128)(2,1)} fusion(bf16[6144,1024]{0,1:T(8,128)(2,1)} %fusion.3, bf16[1024,128]{1,0:T(8,128)(2,1)S(1)} %convolution_convert_fusion.4, bf16[8,6144,128]{2,1,0:T(8,128)(2,1)} %param.4), kind=kOutput, calls=%fused_computation.5 | convolution fusion | flops 1629487104 | bytes 27000832 | tf_op jit(solution)/shard_map/dot_general | solution.py:37
  314.3 1.8 convolution_convert_fusion.3
  321.1 9.8 %fusion.1 = bf16[6144,1024]{0,1:T(8,128)(2,1)} fusion(bf16[6144,1024]{0,1:T(8,128)(2,1)} %fusion.2, bf16[1024,128]{1,0:T(8,128)(2,1)S(1)} %convolution_convert_fusion.3, bf16[8,6144,128]{2,1,0:T(8,128)(2,1)} %param.4), kind=kOutput, calls=%fused_computation.3 | convolution fusion | flops 1629487104 | bytes 27000832 | tf_op jit(solution)/shard_map/dot_general | solution.py:37
  332.0 1.8 convolution_convert_fusion.2
  333.8 10.1 %multiply_reduce_fusion = (f32[1024]{0:T(1024)S(1)}, bf16[6144,1024]{0,1:T(8,128)(2,1)}) fusion(bf16[1024,128]{1,0:T(8,128)(2,1)S(1)} %convolution_convert_fusion.2, bf16[8,6144,128]{2,1,0:T(8,128)(2,1)} %param.4, bf16[6144,1024]{0,1:T(8,128)(2,1)} %fusion.1), kind=kOutput, calls=%fused_computation.16 | convolution fusion | flops 1648360448 | bytes 27004928 | tf_op jit(solution)/shard_map/dot_general | solution.py:37
  343.9 16.6 %copy.9 = bf16[6144,1024]{1,0:T(8,128)(2,1)} copy(bf16[6144,1024]{0,1:T(8,128)(2,1)} %get-tuple-element.9) | data formatting | bytes 25165824
  360.5 19.1 %psum.23 = f32[1024]{0:T(1024)S(1)} all-reduce(f32[1024]{0:T(1024)S(1)} %get-tuple-element.8), channel_id=1, replica_groups=mesh['row'=8,'col'=4] {'row'}, use_global_device_ids=true, to_apply=%region_3.0 | all-reduce | flops 1024 | bytes 8192 | tf_op jit(solution)/shard_map/psum | solution.py:41
  (35 shorter events, 29.8 us)
Async XLA Ops:
  7.2 211.8 %all-reduce.3.cloned.1.call-start = ((), (), s32[]{:S(2)}) async-start(), calls=%async_computation | async-start | bytes 8388608 | tf_op jit(solution)/shard_map/psum | solution.py:22
  23.8 19.0 %copy-start = (bf16[6144,1024]{1,0:T(8,128)(2,1)S(1)}, bf16[6144,1024]{1,0:T(8,128)(2,1)}, u32[]{:S(2)}) copy-start(bf16[6144,1024]{1,0:T(8,128)(2,1)} %param.3) | copy-start | bytes 37748740
  256.6 9.9 %copy-start.1 = (f32[128,1024]{1,0:T(8,128)S(1)}, f32[128,1024]{1,0:T(8,128)}, u32[]{:S(2)}) copy-start(f32[128,1024]{1,0:T(8,128)} %convolution_subtract_fusion.23) | copy-start | bytes 1572868
Sparse Core Ops, SparseCore 0:
  59.9 159.1 all-reduce.2
where the time goes:
time: 391 us; the launch traced here: 387 us
  matrix products  158 us (40%)
  waiting for transfers between devices  143 us (37%)
  local copies, waits for them, and re-layouts  49.4 us (13%)
  blocking collectives  19.1 us (5%)
  between operations  14.3 us (4%)
    psum x1, waiting for transfers between devices, body(): lax.psum(local_proj.astype(jnp.bfloat16), 'row').astype(jnp.float32)  143 us
    dot_general x8, matrix products, body(): jnp.dot(reflectors[panel], scaled, preferred_element_type=jnp.float32)  78.9 us
    unnamed x7, local copies, waits for them, and re-layouts  49.4 us
    dot_general x28, matrix products, body(): jnp.dot(cross, earlier[prior].astype(jnp.float32), precision=lax.Precisio...  29.5 us
    psum x1, blocking collectives, body(): squares = lax.psum(local_squares, 'row')  19.1 us
    dot_general x1, matrix products, body(): lax.dot_general(stacked, stacked, (((0,), (0,)), ((), ())), preferred_ele...  19 us
    dot_general x1, matrix products, body(): lax.dot_general(stacked, eigvecs, (((0,), (0,)), ((), ())), preferred_ele...  16.9 us
    dot_general x8, matrix products, body(): jnp.dot(factors[panel], proj, precision=lax.Precision.HIGHEST)  14.3 us
  transfers between devices with their start and end apart: 1, of which 1 were waited for; matrix products, arithmetic and copies ran while one was open for 4% of the time, Pallas kernels for 0%

commit v1 on v0

--- a/solution.py
+++ b/solution.py
@@ -19,7 +19,7 @@
         stacked, stacked, (((0,), (0,)), ((), ())), preferred_element_type=jnp.float32
     )
     total_proj, total_gram = (
-        lax.psum(local_proj.astype(jnp.bfloat16), "row").astype(jnp.float32),
+        jnp.sum(lax.all_gather(local_proj.astype(jnp.bfloat16), "row"), axis=0).astype(jnp.float32),
         lax.psum(local_gram.astype(jnp.bfloat16), "row").astype(jnp.float32),
     )
     earlier = []

time: 391 us -> 539 us (1.38)
  waiting for transfers between devices: 143 us -> 286 us
  other arithmetic: 2.64 us -> 12.7 us
    all_gather x0 -> x1, waiting for transfers between devices: none -> 194 us  [body(): lax.all_gather(local_proj.astype(jnp.bfloat16), 'row')]
    psum x1, waiting for transfers between devices: 143 us -> 91.6 us  [body(): lax.psum(local_gram.astype(jnp.bfloat16), 'row').astype(jnp.float32)]
    reduce_sum x0 -> x1, other arithmetic: none -> 9.67 us  [body(): jnp.sum(lax.all_gather(local_proj.astype(jnp.bfloat16), 'row'), axis=0)]
    dot_general x8, matrix products: 14.3 us -> 7.41 us  [body(): jnp.dot(factors[panel], proj, precision=lax.Precision.HIGHEST)]
    unnamed x7 -> x5, local copies, waits for them, and re-layouts: 49.4 us -> 49.8 us
  transfers between devices with their start and end apart: 1 -> 2, of which waited for: 1 -> 2; matrix products, arithmetic and copies ran while one was open for 4% -> 9% of each run, Pallas kernels for 0% -> 0%
where the time goes in v1:
time: 539 us; the launch traced here: 536 us
  waiting for transfers between devices  286 us (53%)
  matrix products  153 us (28%)
  local copies, waits for them, and re-layouts  49.8 us (9%)
  blocking collectives  19.6 us (4%)
  between operations  14.3 us (3%)
  other arithmetic  12.7 us (2%)
    all_gather x1, waiting for transfers between devices, body(): lax.all_gather(local_proj.astype(jnp.bfloat16), 'row')  194 us
    psum x1, waiting for transfers between devices, body(): lax.psum(local_gram.astype(jnp.bfloat16), 'row').astype(jnp.float32)  91.6 us
    dot_general x8, matrix products, body(): jnp.dot(reflectors[panel], scaled, preferred_element_type=jnp.float32)  78.8 us
    unnamed x5, local copies, waits for them, and re-layouts  49.8 us
    dot_general x28, matrix products, body(): jnp.dot(cross, earlier[prior].astype(jnp.float32), precision=lax.Precisio...  29.7 us
    psum x1, blocking collectives, body(): squares = lax.psum(local_squares, 'row')  19.6 us
    dot_general x1, matrix products, body(): lax.dot_general(stacked, stacked, (((0,), (0,)), ((), ())), preferred_ele...  18.8 us
    dot_general x1, matrix products, body(): lax.dot_general(stacked, eigvecs, (((0,), (0,)), ((), ())), preferred_ele...  18.7 us
  transfers between devices with their start and end apart: 2, of which 2 were waited for; matrix products, arithmetic and copies ran while one was open for 9% of the time, Pallas kernels for 0%

profile of v1, /device:TPU:0, one launch (start us, length us, event | category | flops | bytes accessed | tf_op | source)
XLA Modules:
  0.0 536.3 jit_solution(6553943589801509986)
XLA Ops:
  7.2 16.6 %copy.8 = bf16[8,6144,128]{1,2,0:T(8,128)(2,1)} copy(bf16[8,6144,128]{2,1,0:T(8,128)(2,1)} %param.4) | data formatting | bytes 25165824 | tf_op args[1]
  23.8 18.7 %convolution_convert_fusion.1 = bf16[1024,1024]{1,0:T(8,128)(2,1)} fusion(bf16[6144,1024]{0,1:T(8,128)(2,1)} %bitcast.134, bf16[6144,1024]{1,0:T(8,128)(2,1)} %param.3), kind=kOutput, calls=%fused_computation.18 | convolution fusion | flops 12885950464 | bytes 27262976 | tf_op jit(solution)/shard_map/dot_general | solution.py:15
  42.8 18.8 %convolution_convert_fusion = bf16[1024,1024]{1,0:T(8,128)(2,1)} fusion(bf16[6144,1024]{0,1:T(8,128)(2,1)} %bitcast.135), kind=kOutput, calls=%fused_computation.17 | convolution fusion | flops 12885950464 | bytes 14680064 | tf_op jit(solution)/shard_map/dot_general | solution.py:18
  61.6 16.6 %copy.7 = bf16[6144,1024]{0,1:T(8,128)(2,1)} copy(bf16[6144,1024]{1,0:T(8,128)(2,1)} %param.3) | data formatting | bytes 25165824 | tf_op args[0]
  78.2 194.5 %all-gather.3.cloned.1.call-done = bf16[8192,1024]{1,0:T(8,128)(2,1)} async-done(((bf16[1024,1024]{1,0:T(8,128)(2,1)}), bf16[8192,1024]{1,0:T(8,128)(2,1)}) %all-gather.3.cloned.1.call-update) | async-done | bytes 16777232 | tf_op jit(solution)/shard_map/all_gather | solution.py:22
  272.7 9.7 %reduce_sum.21 = bf16[1024,1024]{1,0:T(8,128)(2,1)S(1)} reduce(bf16[8,1024,1024]{2,1,0:T(8,128)(2,1)} %bitcast.133, bf16[]{:T(256)} %constant.6.clone.1), dimensions={0}, to_apply=%region_0.0 | reduce | flops 7340032 | bytes 18874370 | tf_op jit(solution)/shard_map/reduce_sum | solution.py:22
  282.4 2.4 convert_element_type.128
  285.2 91.6 %all-reduce.2.cloned.1.call-done = bf16[1024,1024]{1,0:T(8,128)(2,1)} async-done(((bf16[1024,1024]{1,0:T(8,128)(2,1)}), bf16[1024,1024]{1,0:T(8,128)(2,1)}) %all-reduce.2.cloned.1.call-update) | async-done | bytes 2097168 | tf_op jit(solution)/shard_map/psum | solution.py:23
  379.1 1.3 convolution_subtract_fusion.26
  382.4 9.8 %fusion.7 = bf16[6144,1024]{0,1:T(8,128)(2,1)} fusion(bf16[6144,1024]{0,1:T(8,128)(2,1)} %copy.7, bf16[1024,128]{1,0:T(8,128)(2,1)S(1)} %convolution_convert_fusion.9, bf16[8,6144,128]{2,1,0:T(8,128)(2,1)} %param.4), kind=kOutput, calls=%fused_computation.15 | convolution fusion | flops 1629487104 | bytes 27000832 | tf_op jit(solution)/shard_map/dot_general | solution.py:37
  392.3 9.8 %fusion.6 = bf16[6144,1024]{0,1:T(8,128)(2,1)} fusion(bf16[6144,1024]{0,1:T(8,128)(2,1)} %fusion.7, bf16[1024,128]{1,0:T(8,128)(2,1)S(1)} %convolution_convert_fusion.8, bf16[8,6144,128]{2,1,0:T(8,128)(2,1)} %param.4), kind=kOutput, calls=%fused_computation.13 | convolution fusion | flops 1629487104 | bytes 27000832 | tf_op jit(solution)/shard_map/dot_general | solution.py:37
  402.1 9.8 %fusion.5 = bf16[6144,1024]{0,1:T(8,128)(2,1)} fusion(bf16[6144,1024]{0,1:T(8,128)(2,1)} %fusion.6, bf16[1024,128]{1,0:T(8,128)(2,1)S(1)} %convolution_convert_fusion.7, bf16[8,6144,128]{2,1,0:T(8,128)(2,1)} %param.4), kind=kOutput, calls=%fused_computation.11 | convolution fusion | flops 1629487104 | bytes 27000832 | tf_op jit(solution)/shard_map/dot_general | solution.py:37
  411.9 1.3 convolution_subtract_fusion.24
  416.1 9.8 %fusion.4 = bf16[6144,1024]{0,1:T(8,128)(2,1)} fusion(bf16[6144,1024]{0,1:T(8,128)(2,1)} %fusion.5, bf16[1024,128]{1,0:T(8,128)(2,1)S(1)} %convolution_convert_fusion.6, bf16[8,6144,128]{2,1,0:T(8,128)(2,1)} %param.4), kind=kOutput, calls=%fused_computation.9 | convolution fusion | flops 1629487104 | bytes 27000832 | tf_op jit(solution)/shard_map/dot_general | solution.py:37
  426.0 1.3 convolution_subtract_fusion.21
  431.2 9.8 %fusion.3 = bf16[6144,1024]{0,1:T(8,128)(2,1)} fusion(bf16[6144,1024]{0,1:T(8,128)(2,1)} %fusion.4, bf16[1024,128]{1,0:T(8,128)(2,1)S(1)} %convolution_convert_fusion.5, bf16[8,6144,128]{2,1,0:T(8,128)(2,1)} %param.4), kind=kOutput, calls=%fused_computation.7 | convolution fusion | flops 1629487104 | bytes 27000832 | tf_op jit(solution)/shard_map/dot_general | solution.py:37
  441.1 1.3 convolution_subtract_fusion.17
  447.3 9.8 %fusion.2 = bf16[6144,1024]{0,1:T(8,128)(2,1)} fusion(bf16[6144,1024]{0,1:T(8,128)(2,1)} %fusion.3, bf16[1024,128]{1,0:T(8,128)(2,1)S(1)} %convolution_convert_fusion.4, bf16[8,6144,128]{2,1,0:T(8,128)(2,1)} %param.4), kind=kOutput, calls=%fused_computation.5 | convolution fusion | flops 1629487104 | bytes 27000832 | tf_op jit(solution)/shard_map/dot_general | solution.py:37
  457.2 1.3 convolution_subtract_fusion.12
  464.4 9.8 %fusion.1 = bf16[6144,1024]{0,1:T(8,128)(2,1)} fusion(bf16[6144,1024]{0,1:T(8,128)(2,1)} %fusion.2, bf16[1024,128]{1,0:T(8,128)(2,1)S(1)} %convolution_convert_fusion.3, bf16[8,6144,128]{2,1,0:T(8,128)(2,1)} %param.4), kind=kOutput, calls=%fused_computation.3 | convolution fusion | flops 1629487104 | bytes 27000832 | tf_op jit(solution)/shard_map/dot_general | solution.py:37
  474.2 1.3 convolution_subtract_fusion.6
  482.5 10.1 %multiply_reduce_fusion = (f32[1024]{0:T(1024)S(1)}, bf16[6144,1024]{0,1:T(8,128)(2,1)}) fusion(bf16[1024,128]{1,0:T(8,128)(2,1)S(1)} %convolution_convert_fusion.2, bf16[8,6144,128]{2,1,0:T(8,128)(2,1)} %param.4, bf16[6144,1024]{0,1:T(8,128)(2,1)} %fusion.1), kind=kOutput, calls=%fused_computation.16 | convolution fusion | flops 1648360448 | bytes 27004928 | tf_op jit(solution)/shard_map/dot_general | solution.py:37
  492.7 16.6 %copy.9 = bf16[6144,1024]{1,0:T(8,128)(2,1)} copy(bf16[6144,1024]{0,1:T(8,128)(2,1)} %get-tuple-element.7) | data formatting | bytes 25165824
  509.2 19.6 %psum.15 = f32[1024]{0:T(1024)S(1)} all-reduce(f32[1024]{0:T(1024)S(1)} %get-tuple-element.6), channel_id=1, replica_groups=mesh['row'=8,'col'=4] {'row'}, use_global_device_ids=true, to_apply=%region_3.0 | all-reduce | flops 1024 | bytes 8192 | tf_op jit(solution)/shard_map/psum | solution.py:41
  (37 shorter events, 30.3 us)
Async XLA Ops:
  7.2 265.5 %all-gather.3.cloned.1.call-start = ((), (), s32[]{:S(2)}) async-start(), calls=%async_computation.1 | async-start | bytes 18874368 | tf_op jit(solution)/shard_map/all_gather | solution.py:22
  42.5 334.3 %all-reduce.2.cloned.1.call-start = ((), (), s32[]{:S(2)}) async-start(), calls=%async_computation | async-start | bytes 4194304 | tf_op jit(solution)/shard_map/psum | solution.py:23
  282.4 2.4 copy-start
Sparse Core Ops, SparseCore 0:
  42.7 229.9 all-gather.2
  276.3 100.4 all-reduce.1
